TPU v7x, 32 devices: a whole 2x2x4 slice. The times are simulated.
32 devices in a mesh: rows: 4 (over x, core), cols: 8 (over z, y).
Axes of the slice: x: 2, y: 2, z: 4, core: 2. Of those that a mesh axis runs over, the one named last changes fastest.
Arguments:
- design: bfloat16 [4096, 8192], P('rows', 'cols'), may hold values from -6 to 6
- theta: float32 [8192], P('cols'), may hold values from -0.0625 to 0.0625
- feature_scale: float32 [8192], P('cols'), may hold values from 0.05 to 2
- labels: int32 [4096], P('rows'), may hold values 0 or 1
- psi: bfloat16 [1024, 256], replicated, may hold values from -0.1875 to 0.1875
- phi: float32 [512, 256], replicated, may hold values from -0.25 to 0.25
Outputs:
- newton_step: float32 [8192], P('cols')
- sketch: float32 [256, 8192], P(None, 'cols')
All inputs are finite; a program needn't handle non-finite values. No bound on the sum of `labels` on one device may be relied on, other than what follows from the above.
Results may differ from a plain program's by a relative error of at most 0.0085.
Values sent between devices are 32-bit elements; how exact they have to be, the bound alone decides.
No kernel may reach another device: no remote copies, remote signals or barrier semaphores. Data moves between devices by JAX's collectives and lax.ppermute only.
A program may use at most 128 MiB of HBM per device.

v0:
```python
import jax
import jax.numpy as jnp
from jax import lax
from jax.sharding import PartitionSpec as P

ITERS = 10
damping = 0.01
shrink_share = 0.05
highest = lax.Precision.HIGHEST


def swapped(value, axis, stride):
    mask = 2**stride
    pairs = [(source, source ^ mask) for source in range(lax.axis_size(axis))]
    return lax.ppermute(value, axis, pairs)


def shrink_weights(range_rows):
    width = range_rows.shape[1]
    moment = jnp.dot(range_rows.T, range_rows, precision=highest)
    ridge = shrink_share * jnp.trace(moment) / width
    factor = jnp.linalg.cholesky(moment + ridge * jnp.eye(width, dtype=jnp.float32))
    return jax.scipy.linalg.solve_triangular(factor, range_rows.T, lower=True)


def on_device(design, theta, feature_scale, labels, psi, phi):
    row_devices = lax.axis_size("rows")
    samples = design.shape[0] * row_devices
    width = psi.shape[1]
    scaled_theta = (theta * feature_scale).astype(jnp.bfloat16)
    margins = lax.psum(jnp.dot(design, scaled_theta, preferred_element_type=jnp.float32), "cols")
    chance = jax.nn.sigmoid(margins)
    weight = chance * (1.0 - chance)
    misfit = (chance - labels.astype(jnp.float32)).astype(jnp.bfloat16)
    summed_grad = lax.psum(jnp.dot(misfit, design, preferred_element_type=jnp.float32), "rows")
    gradient = feature_scale * summed_grad / samples + damping * theta
    rows_scaled = (
        design.astype(jnp.float32) * jnp.sqrt(weight)[:, None] * feature_scale[None, :]
    ).astype(jnp.bfloat16)
    mixed_cols = jnp.einsum(
        "rf,rs->fs", rows_scaled, psi, preferred_element_type=jnp.float32
    ).astype(jnp.bfloat16)
    range_rows = lax.psum(
        jnp.dot(rows_scaled, mixed_cols, preferred_element_type=jnp.float32), "cols"
    )
    leaf_weights = shrink_weights(range_rows).astype(jnp.bfloat16)
    sketch = jnp.dot(leaf_weights, rows_scaled, preferred_element_type=jnp.float32)
    position = lax.axis_index("rows")
    for level_bit in range(row_devices.bit_length() - 1):
        partner = swapped(sketch, "rows", level_bit)
        first_low = position // (1 << level_bit) % 2 == 0
        lower_half = jnp.where(first_low, sketch, partner)
        upper_half = jnp.where(first_low, partner, sketch)
        stacked = jnp.concatenate([lower_half, upper_half], 0)
        gram = lax.psum(jnp.dot(stacked, stacked.T, precision=highest), "cols")
        range_rows = jnp.dot(gram, phi, precision=highest)
        sketch = jnp.dot(shrink_weights(range_rows), stacked, precision=highest)
    kernel_part = lax.psum(jnp.dot(sketch, sketch.T, precision=highest), "cols")
    kernel = kernel_part + damping * samples * jnp.eye(width, dtype=jnp.float32)
    kernel_factor = jnp.linalg.cholesky(kernel)
    solution = jnp.zeros_like(gradient)
    residual = gradient

    def precondition_plus(vector):
        projected, squared = lax.psum(
            (jnp.dot(sketch, vector, precision=highest), jnp.sum(vector * vector)), "cols"
        )
        solved = jax.scipy.linalg.cho_solve((kernel_factor, True), projected)
        smoothed = (vector - jnp.dot(solved, sketch, precision=highest)) / damping
        return (smoothed, (squared - jnp.sum(projected * solved)) / damping)

    search, agreement = precondition_plus(residual)
    for turn_index in range(ITERS):
        rounded = (feature_scale * search).astype(jnp.bfloat16)
        forward_rows, length = lax.psum(
            (
                jnp.dot(design, rounded, preferred_element_type=jnp.float32),
                jnp.sum(search * search),
            ),
            "cols",
        )
        inner = (weight * forward_rows).astype(jnp.bfloat16)
        back_sum, bending = lax.psum(
            (
                jnp.dot(inner, design, preferred_element_type=jnp.float32),
                jnp.sum(forward_rows * inner.astype(jnp.float32)),
            ),
            "rows",
        )
        product = feature_scale * back_sum / samples + damping * search
        product, curvature = (product, bending / samples + damping * length)
        step_size = agreement / curvature
        solution = solution + step_size * search
        residual = residual - step_size * product
        if turn_index + 1 < ITERS:
            smoothed, agreement_next = precondition_plus(residual)
            search = smoothed + agreement_next / agreement * search
            agreement = agreement_next
    return (solution, sketch)


def solution(mesh):
    in_specs = (P("rows", "cols"), P("cols"), P("cols"), P("rows"), P(), P())
    out_specs = (P("cols"), P(None, "cols"))
    return jax.shard_map(
        on_device, mesh=mesh, in_specs=in_specs, out_specs=out_specs, check_vma=False
    )
```

profile of v0, /device:TPU:0, one launch (start us, length us, event | category | flops | bytes accessed | tf_op | source)
XLA Modules:
  0.0 1237.9 jit_solution(12997754419069925355)
XLA Ops:
  10.4 23.2 %psum.455 = f32[1024]{0:T(1024)S(1)} all-reduce(f32[1024]{0:T(1024)S(1)} %bitcast.779), channel_id=1, replica_groups=mesh['rows'=4,'cols'=8] {'cols'}, use_global_device_ids=true, to_apply=%region_0.0 | all-reduce | flops 1024 | bytes 8192 | tf_op jit(solution)/shard_map/psum | solution.py:31
  33.6 3.3 fusion.44
  38.1 74.6 %all-reduce.34.cloned.1.call-done = f32[1024,256]{1,0:T(8,128)} async-done(((f32[1024,256]{1,0:T(8,128)}), f32[1024,256]{1,0:T(8,128)}) %all-reduce.34.cloned.1.call-update) | async-done | bytes 1048592 | tf_op jit(solution)/shard_map/psum | solution.py:43
  112.7 4.0 select_reduce_fusion.2
  117.6 11.7 cholesky.214
  129.3 9.8 custom-call.34
  139.6 11.7 cholesky.231
  154.5 4.3 while.25
  158.9 19.7 %custom-call.20 = f32[2,128,128]{1,2,0:T(8,128)S(1)} custom-call(f32[2,128,128]{2,1,0:T(8,128)S(1)} %get-tuple-element.28), custom_call_target="InvertDiagBlocksLowerTriangular" | custom-call | tf_op jit(solution)/shard_map/jit(_solve_triangular)/triangular_solve | solution.py:23
  184.8 3.0 collective-permute-done
  190.9 4.5 fusion.3
  195.7 77.8 %all-reduce.36.cloned.1.call-done = f32[512,512]{1,0:T(8,128)} async-done(((f32[512,512]{1,0:T(8,128)}), f32[512,512]{1,0:T(8,128)}) %all-reduce.36.cloned.1.call-update) | async-done | bytes 1048592 | tf_op jit(solution)/shard_map/psum | solution.py:55
  282.5 11.7 cholesky.248
  294.3 10.4 custom-call.35
  306.9 12.1 cholesky.265
  322.6 5.4 while.26
  328.7 20.5 %custom-call.36 = f32[2,128,128]{1,2,0:T(8,128)S(1)} custom-call(f32[2,128,128]{2,1,0:T(8,128)} %copy-done.15), custom_call_target="InvertDiagBlocksLowerTriangular" | custom-call | tf_op jit(solution)/shard_map/jit(_solve_triangular)/triangular_solve | solution.py:23
  350.6 4.1 fusion.2
  356.2 23.7 %collective-permute-done.1 = f32[256,1024]{1,0:T(8,128)} collective-permute-done((f32[256,1024]{1,0:T(8,128)}, f32[256,1024]{1,0:T(8,128)}, u32[]{:S(2)}, u32[]{:S(2)}) %collective-permute-start.1) | collective-permute-done | bytes 1048608 | tf_op jit(solution)/shard_map/ppermute | solution.py:15
  382.9 4.5 fusion.1
  387.9 5.8 psum.456
  393.7 71.1 %all-reduce.38.cloned.1.call-done = f32[512,512]{1,0:T(8,128)} async-done(((f32[512,512]{1,0:T(8,128)}), f32[512,512]{1,0:T(8,128)}) %all-reduce.38.cloned.1.call-update) | async-done | bytes 1048592 | tf_op jit(solution)/shard_map/psum | solution.py:55
  473.8 11.7 cholesky.282
  485.6 10.4 custom-call.37
  498.2 11.9 cholesky.299
  513.7 5.4 while.27
  519.8 20.5 %custom-call.38 = f32[2,128,128]{1,2,0:T(8,128)S(1)} custom-call(f32[2,128,128]{2,1,0:T(8,128)} %copy-done.16), custom_call_target="InvertDiagBlocksLowerTriangular" | custom-call | tf_op jit(solution)/shard_map/jit(_solve_triangular)/triangular_solve | solution.py:23
  541.8 3.1 fusion
  550.5 20.5 %psum.461 = f32[256]{0:T(256)S(1)} all-reduce(f32[256]{0:T(256)S(1)} %bitcast.781), channel_id=1, replica_groups=mesh['rows'=4,'cols'=8] {'cols'}, use_global_device_ids=true, to_apply=%region_13.16 | all-reduce | flops 256 | bytes 2048 | tf_op jit(solution)/shard_map/psum | solution.py:65
  571.0 47.4 %all-reduce.40.cloned.1.call-done = f32[256,256]{0,1:T(8,128)} async-done(((f32[256,256]{0,1:T(8,128)}), f32[256,256]{0,1:T(8,128)}) %all-reduce.40.cloned.1.call-update) | async-done | bytes 262160 | tf_op jit(solution)/shard_map/psum | solution.py:58
  620.5 11.7 cholesky.316
  632.3 9.8 custom-call.39
  642.6 11.7 cholesky.333
  657.0 5.4 while.28
  662.5 19.8 %custom-call.40 = f32[2,128,128]{1,2,0:T(8,128)S(1)} custom-call(f32[2,128,128]{2,1,0:T(8,128)S(1)} %get-tuple-element.91), custom_call_target="InvertDiagBlocksLowerTriangular" | custom-call | tf_op jit(solution)/shard_map/jit(_cho_solve)/triangular_solve | solution.py:68
  686.6 20.6 %all-reduce.19 = (f32[1024]{0:T(1024)S(1)}, f32[]{:T(128)}, f32[]{:T(128)}) all-reduce(f32[1024]{0:T(1024)S(1)} %bitcast.760, f32[]{:T(128)} %get-tuple-element.250, f32[]{:T(128)} %get-tuple-element.248), channel_id=1, replica_groups=mesh['rows'=4,'cols'=8] {'cols'}, use_global_device_ids=true, to_apply=%region_17.21 | all-reduce | flops 1026 | bytes 8208 | tf_op jit(solution)/shard_map/psum | solution.py:75
  708.8 6.4 all-reduce.28
  720.6 17.8 %all-reduce.18 = (f32[256]{0:T(256)S(1)}, f32[]{:T(128)}) all-reduce(f32[256]{0:T(256)S(1)} %bitcast.792, f32[]{:T(128)} %get-tuple-element.244), channel_id=1, replica_groups=mesh['rows'=4,'cols'=8] {'cols'}, use_global_device_ids=true, to_apply=%region_25.29 | all-reduce | flops 257 | bytes 2056 | tf_op jit(solution)/shard_map/psum | solution.py:65
  744.7 20.0 %all-reduce.17 = (f32[1024]{0:T(1024)S(1)}, f32[]{:T(128)}) all-reduce(f32[1024]{0:T(1024)S(1)} %bitcast.762, f32[]{:T(128)} %get-tuple-element.242), channel_id=1, replica_groups=mesh['rows'=4,'cols'=8] {'cols'}, use_global_device_ids=true, to_apply=%region_27.31 | all-reduce | flops 1025 | bytes 8200 | tf_op jit(solution)/shard_map/psum | solution.py:75
  765.7 6.4 all-reduce.27
  776.2 17.8 %all-reduce.16 = (f32[256]{0:T(256)S(1)}, f32[]{:T(128)}) all-reduce(f32[256]{0:T(256)S(1)} %bitcast.793, f32[]{:T(128)} %get-tuple-element.238), channel_id=1, replica_groups=mesh['rows'=4,'cols'=8] {'cols'}, use_global_device_ids=true, to_apply=%region_35.39 | all-reduce | flops 257 | bytes 2056 | tf_op jit(solution)/shard_map/psum | solution.py:65
  800.3 20.0 %all-reduce.15 = (f32[1024]{0:T(1024)S(1)}, f32[]{:T(128)}) all-reduce(f32[1024]{0:T(1024)S(1)} %bitcast.764, f32[]{:T(128)} %get-tuple-element.236), channel_id=1, replica_groups=mesh['rows'=4,'cols'=8] {'cols'}, use_global_device_ids=true, to_apply=%region_37.41 | all-reduce | flops 1025 | bytes 8200 | tf_op jit(solution)/shard_map/psum | solution.py:75
  821.4 6.4 all-reduce.26
  831.8 18.0 %all-reduce.14 = (f32[256]{0:T(256)S(1)}, f32[]{:T(128)}) all-reduce(f32[256]{0:T(256)S(1)} %bitcast.794, f32[]{:T(128)} %get-tuple-element.232), channel_id=1, replica_groups=mesh['rows'=4,'cols'=8] {'cols'}, use_global_device_ids=true, to_apply=%region_45.49 | all-reduce | flops 257 | bytes 2056 | tf_op jit(solution)/shard_map/psum | solution.py:65
  857.7 20.0 %all-reduce.13 = (f32[1024]{0:T(1024)S(1)}, f32[]{:T(128)}) all-reduce(f32[1024]{0:T(1024)S(1)} %bitcast.766, f32[]{:T(128)} %get-tuple-element.230), channel_id=1, replica_groups=mesh['rows'=4,'cols'=8] {'cols'}, use_global_device_ids=true, to_apply=%region_47.51 | all-reduce | flops 1025 | bytes 8200 | tf_op jit(solution)/shard_map/psum | solution.py:75
  878.8 6.4 all-reduce.25
  889.3 17.8 %all-reduce.12 = (f32[256]{0:T(256)S(1)}, f32[]{:T(128)}) all-reduce(f32[256]{0:T(256)S(1)} %bitcast.795, f32[]{:T(128)} %get-tuple-element.226), channel_id=1, replica_groups=mesh['rows'=4,'cols'=8] {'cols'}, use_global_device_ids=true, to_apply=%region_55.59 | all-reduce | flops 257 | bytes 2056 | tf_op jit(solution)/shard_map/psum | solution.py:65
  915.0 20.0 %all-reduce.11 = (f32[1024]{0:T(1024)S(1)}, f32[]{:T(128)}) all-reduce(f32[1024]{0:T(1024)S(1)} %bitcast.768, f32[]{:T(128)} %get-tuple-element.224), channel_id=1, replica_groups=mesh['rows'=4,'cols'=8] {'cols'}, use_global_device_ids=true, to_apply=%region_57.61 | all-reduce | flops 1025 | bytes 8200 | tf_op jit(solution)/shard_map/psum | solution.py:75
  936.1 6.4 all-reduce.24
  946.5 17.8 %all-reduce.10 = (f32[256]{0:T(256)S(1)}, f32[]{:T(128)}) all-reduce(f32[256]{0:T(256)S(1)} %bitcast.796, f32[]{:T(128)} %get-tuple-element.220), channel_id=1, replica_groups=mesh['rows'=4,'cols'=8] {'cols'}, use_global_device_ids=true, to_apply=%region_65.69 | all-reduce | flops 257 | bytes 2056 | tf_op jit(solution)/shard_map/psum | solution.py:65
  972.2 20.0 %all-reduce.9 = (f32[1024]{0:T(1024)S(1)}, f32[]{:T(128)}) all-reduce(f32[1024]{0:T(1024)S(1)} %bitcast.770, f32[]{:T(128)} %get-tuple-element.218), channel_id=1, replica_groups=mesh['rows'=4,'cols'=8] {'cols'}, use_global_device_ids=true, to_apply=%region_67.71 | all-reduce | flops 1025 | bytes 8200 | tf_op jit(solution)/shard_map/psum | solution.py:75
  993.3 6.4 all-reduce.23
  1003.8 17.8 %all-reduce.8 = (f32[256]{0:T(256)S(1)}, f32[]{:T(128)}) all-reduce(f32[256]{0:T(256)S(1)} %bitcast.797, f32[]{:T(128)} %get-tuple-element.214), channel_id=1, replica_groups=mesh['rows'=4,'cols'=8] {'cols'}, use_global_device_ids=true, to_apply=%region_75.79 | all-reduce | flops 257 | bytes 2056 | tf_op jit(solution)/shard_map/psum | solution.py:65
  1029.5 20.0 %all-reduce.7 = (f32[1024]{0:T(1024)S(1)}, f32[]{:T(128)}) all-reduce(f32[1024]{0:T(1024)S(1)} %bitcast.772, f32[]{:T(128)} %get-tuple-element.212), channel_id=1, replica_groups=mesh['rows'=4,'cols'=8] {'cols'}, use_global_device_ids=true, to_apply=%region_77.81 | all-reduce | flops 1025 | bytes 8200 | tf_op jit(solution)/shard_map/psum | solution.py:75
  1050.6 6.5 all-reduce.22
  1061.2 18.0 %all-reduce.6 = (f32[256]{0:T(256)S(1)}, f32[]{:T(128)}) all-reduce(f32[256]{0:T(256)S(1)} %bitcast.798, f32[]{:T(128)} %get-tuple-element.208), channel_id=1, replica_groups=mesh['rows'=4,'cols'=8] {'cols'}, use_global_device_ids=true, to_apply=%region_85.89 | all-reduce | flops 257 | bytes 2056 | tf_op jit(solution)/shard_map/psum | solution.py:65
  1087.1 20.0 %all-reduce.5 = (f32[1024]{0:T(1024)S(1)}, f32[]{:T(128)}) all-reduce(f32[1024]{0:T(1024)S(1)} %bitcast.774, f32[]{:T(128)} %get-tuple-element.206), channel_id=1, replica_groups=mesh['rows'=4,'cols'=8] {'cols'}, use_global_device_ids=true, to_apply=%region_87.91 | all-reduce | flops 1025 | bytes 8200 | tf_op jit(solution)/shard_map/psum | solution.py:75
  1108.2 6.5 all-reduce.21
  1118.8 17.8 %all-reduce.4 = (f32[256]{0:T(256)S(1)}, f32[]{:T(128)}) all-reduce(f32[256]{0:T(256)S(1)} %bitcast.799, f32[]{:T(128)} %get-tuple-element.202), channel_id=1, replica_groups=mesh['rows'=4,'cols'=8] {'cols'}, use_global_device_ids=true, to_apply=%region_95.99 | all-reduce | flops 257 | bytes 2056 | tf_op jit(solution)/shard_map/psum | solution.py:65
  1144.5 20.0 %all-reduce.3 = (f32[1024]{0:T(1024)S(1)}, f32[]{:T(128)}) all-reduce(f32[1024]{0:T(1024)S(1)} %bitcast.776, f32[]{:T(128)} %get-tuple-element.200), channel_id=1, replica_groups=mesh['rows'=4,'cols'=8] {'cols'}, use_global_device_ids=true, to_apply=%region_97.101 | all-reduce | flops 1025 | bytes 8200 | tf_op jit(solution)/shard_map/psum | solution.py:75
  1165.5 6.5 all-reduce.20
  1176.1 17.8 %all-reduce.2 = (f32[256]{0:T(256)S(1)}, f32[]{:T(128)}) all-reduce(f32[256]{0:T(256)S(1)} %bitcast.800, f32[]{:T(128)} %get-tuple-element.196), channel_id=1, replica_groups=mesh['rows'=4,'cols'=8] {'cols'}, use_global_device_ids=true, to_apply=%region_105.109 | all-reduce | flops 257 | bytes 2056 | tf_op jit(solution)/shard_map/psum | solution.py:65
  1201.9 20.0 %all-reduce.1 = (f32[1024]{0:T(1024)S(1)}, f32[]{:T(128)}) all-reduce(f32[1024]{0:T(1024)S(1)} %bitcast.778, f32[]{:T(128)} %get-tuple-element.194), channel_id=1, replica_groups=mesh['rows'=4,'cols'=8] {'cols'}, use_global_device_ids=true, to_apply=%region_107.111 | all-reduce | flops 1025 | bytes 8200 | tf_op jit(solution)/shard_map/psum | solution.py:75
  1222.6 6.5 psum.518
  (338 shorter events, 177.8 us)
Async XLA Ops:
  7.2 26.4 %copy-start = (bf16[1024,256]{1,0:T(8,128)(2,1)S(1)}, bf16[1024,256]{1,0:T(8,128)(2,1)}, u32[]{:S(2)}) copy-start(bf16[1024,256]{1,0:T(8,128)(2,1)} %param.15) | copy-start | bytes 1572868
  7.2 26.4 %copy-start.10 = (f32[1024]{0:T(1024)S(1)}, f32[1024]{0:T(1024)}, u32[]{:S(2)}) copy-start(f32[1024]{0:T(1024)} %param.13) | copy-start | bytes 12292
  7.2 26.4 %copy-start.1 = (bf16[1024,1024]{1,0:T(8,128)(2,1)S(1)}, bf16[1024,1024]{1,0:T(8,128)(2,1)}, u32[]{:S(2)}) copy-start(bf16[1024,1024]{1,0:T(8,128)(2,1)} %param.11) | copy-start | bytes 6291460
  7.2 26.3 %copy-start.18 = (s32[1024]{0:T(1024)S(1)}, s32[1024]{0:T(1024)}, u32[]{:S(2)}) copy-start(s32[1024]{0:T(1024)} %param.14) | copy-start | bytes 12292
  7.2 105.5 %all-reduce.34.cloned.1.call-start = ((), (), s32[]{:S(2)}) async-start(), calls=%async_computation | async-start | bytes 2097152 | tf_op jit(solution)/shard_map/psum | solution.py:43
  36.9 236.6 %all-reduce.36.cloned.1.call-start = ((), (), s32[]{:S(2)}) async-start(), calls=%async_computation.1 | async-start | bytes 2097152 | tf_op jit(solution)/shard_map/psum | solution.py:55
  158.9 19.7 %copy-start.19 = (s32[2,2]{1,0:T(2,128)}, s32[2,2]{1,0:T(2,128)S(1)}, u32[]{:S(2)}) copy-start(s32[2,2]{1,0:T(2,128)S(1)} %get-tuple-element.492) | copy-start | bytes 52
  184.8 3.0 collective-permute-start
  189.5 1.0 copy-start.7
  189.5 1.3 copy-start.9
  195.4 269.4 %all-reduce.38.cloned.1.call-start = ((), (), s32[]{:S(2)}) async-start(), calls=%async_computation.2 | async-start | bytes 2097152 | tf_op jit(solution)/shard_map/psum | solution.py:55
  281.8 0.7 copy-start.13
  319.0 2.6 copy-start.11
  328.0 0.6 copy-start.15
  349.2 1.5 copy-start.8
  354.7 25.2 %collective-permute-start.1 = (f32[256,1024]{1,0:T(8,128)}, f32[256,1024]{1,0:T(8,128)}, u32[]{:S(2)}, u32[]{:S(2)}) collective-permute-start(f32[256,1024]{1,0:T(8,128)} %fusion.2), channel_id=1, source_target_pairs={{0,16},{8,24},{16,0},{24,8},{1,17},{9,25},{17,1},{25,9},{2,18},{10... | collective-permute-start | bytes 3145736 | tf_op jit(solution)/shard_map/ppermute | solution.py:15
  381.6 1.0 copy-start.4
  381.6 1.3 copy-start.6
  387.5 231.0 %all-reduce.40.cloned.1.call-start = ((), (), s32[]{:S(2)}) async-start(), calls=%async_computation.3 | async-start | bytes 524288 | tf_op jit(solution)/shard_map/psum | solution.py:58
  473.1 0.7 copy-start.14
  510.1 2.6 copy-start.12
  519.2 0.6 copy-start.16
  540.3 1.5 copy-start.5
  544.9 1.0 copy-start.2
  545.9 1.8 copy-start.17
  662.5 132.3 %copy-start.3 = (f32[256,256]{1,0:T(8,128)}, f32[256,256]{1,0:T(8,128)S(1)}, u32[]{:S(2)}) copy-start(f32[256,256]{1,0:T(8,128)S(1)} %get-tuple-element.476) | copy-start | bytes 786436
Sparse Core Ops, SparseCore 0:
  37.0 75.6 all-reduce.33
  195.5 77.9 all-reduce.35
  387.6 77.2 all-reduce.37
  547.8 70.6 all-reduce.39
where the time goes:
time: 1240 us
  blocking collectives  475 us (38%)
  waiting for transfers between devices  298 us (24%)
  other arithmetic  259 us (21%)
  matrix products  123 us (10%)
  between operations  48.4 us (4%)
  local copies, waits for them, and re-layouts  32 us (3%)
    psum x10, blocking collectives, on_device(): lax.psum((jnp.dot(design, rounded, preferred_element_type=jnp.float32), j...  201 us
    psum x10, blocking collectives, precondition_plus(): lax.psum((jnp.dot(sketch, vector, precision=highest), jnp.sum(vector * ve...  181 us
    psum x2, waiting for transfers between devices, on_device(): gram = lax.psum(jnp.dot(stacked, stacked.T, precision=highest), 'cols')  149 us
    another operation x20, other arithmetic, shrink_weights(): jnp.linalg.cholesky(moment + ridge * jnp.eye(width, dtype=jnp.float32))  105 us
    psum x1, waiting for transfers between devices, on_device(): lax.psum(jnp.dot(rows_scaled, mixed_cols, preferred_element_type=jnp.floa...  74.6 us
    psum x10, blocking collectives, on_device(): lax.psum((jnp.dot(inner, design, preferred_element_type=jnp.float32), jnp...  64.5 us
    another operation x7, other arithmetic, shrink_weights(): return jax.scipy.linalg.solve_triangular(factor, range_rows.T, lower=True)  63.2 us
    psum x1, waiting for transfers between devices, on_device(): kernel_part = lax.psum(jnp.dot(sketch, sketch.T, precision=highest), 'cols')  47.4 us
  transfers between devices with their start and end apart: 6, of which 6 were waited for; matrix products, arithmetic and copies ran while one was open for 0% of the time, Pallas kernels for 0%

commit v1 on v0

--- a/solution.py
+++ b/solution.py
@@ -52,7 +52,9 @@
         lower_half = jnp.where(first_low, sketch, partner)
         upper_half = jnp.where(first_low, partner, sketch)
         stacked = jnp.concatenate([lower_half, upper_half], 0)
-        gram = lax.psum(jnp.dot(stacked, stacked.T, precision=highest), "cols")
+        x = jnp.dot(stacked, stacked.T, precision=highest)
+        pieces = lax.all_gather(x, "cols")
+        gram = jnp.sum(pieces, axis=0)
         range_rows = jnp.dot(gram, phi, precision=highest)
         sketch = jnp.dot(shrink_weights(range_rows), stacked, precision=highest)
     kernel_part = lax.psum(jnp.dot(sketch, sketch.T, precision=highest), "cols")

time: 1240 us -> 1350 us (1.089)
  waiting for transfers between devices: 298 us -> 390 us
    all_gather x0 -> x2, waiting for transfers between devices: none -> 241 us  [on_device(): pieces = lax.all_gather(x, 'cols')]
    psum x2 -> x0, waiting for transfers between devices: 149 us -> none  [on_device(): gram = lax.psum(jnp.dot(stacked, stacked.T, precision=highest), 'cols')]
where the time goes in v1:
time: 1350 us; the launch traced here: 1340 us
  blocking collectives  473 us (35%)
  waiting for transfers between devices  390 us (29%)
  other arithmetic  270 us (20%)
  matrix products  123 us (9%)
  between operations  48.4 us (4%)
  local copies, waits for them, and re-layouts  32 us (2%)
    all_gather x2, waiting for transfers between devices, on_device(): pieces = lax.all_gather(x, 'cols')  241 us
    psum x10, blocking collectives, on_device(): lax.psum((jnp.dot(design, rounded, preferred_element_type=jnp.float32), j...  201 us
    psum x10, blocking collectives, precondition_plus(): lax.psum((jnp.dot(sketch, vector, precision=highest), jnp.sum(vector * ve...  179 us
    another operation x20, other arithmetic, shrink_weights(): jnp.linalg.cholesky(moment + ridge * jnp.eye(width, dtype=jnp.float32))  105 us
    psum x1, waiting for transfers between devices, on_device(): lax.psum(jnp.dot(rows_scaled, mixed_cols, preferred_element_type=jnp.floa...  74.6 us
    psum x10, blocking collectives, on_device(): lax.psum((jnp.dot(inner, design, preferred_element_type=jnp.float32), jnp...  64.5 us
    another operation x7, other arithmetic, shrink_weights(): return jax.scipy.linalg.solve_triangular(factor, range_rows.T, lower=True)  63.2 us
    psum x1, waiting for transfers between devices, on_device(): kernel_part = lax.psum(jnp.dot(sketch, sketch.T, precision=highest), 'cols')  47.7 us
  transfers between devices with their start and end apart: 6, of which 6 were waited for; matrix products, arithmetic and copies ran while one was open for 0% of the time, Pallas kernels for 0%

profile of v1, /device:TPU:0, one launch (start us, length us, event | category | flops | bytes accessed | tf_op | source)
XLA Modules:
  0.0 1339.1 jit_solution(1096300679722532463)
XLA Ops:
  10.4 23.2 %psum.441 = f32[1024]{0:T(1024)S(1)} all-reduce(f32[1024]{0:T(1024)S(1)} %bitcast.783), channel_id=1, replica_groups=mesh['rows'=4,'cols'=8] {'cols'}, use_global_device_ids=true, to_apply=%region_0.0 | all-reduce | flops 1024 | bytes 8192 | tf_op jit(solution)/shard_map/psum | solution.py:31
  33.6 3.3 fusion.44
  38.1 74.6 %all-reduce.32.cloned.1.call-done = f32[1024,256]{1,0:T(8,128)} async-done(((f32[1024,256]{1,0:T(8,128)}), f32[1024,256]{1,0:T(8,128)}) %all-reduce.32.cloned.1.call-update) | async-done | bytes 1048592 | tf_op jit(solution)/shard_map/psum | solution.py:43
  112.7 4.0 select_reduce_fusion.2
  117.6 11.7 cholesky.214
  129.3 9.8 custom-call.34
  139.6 11.7 cholesky.231
  154.5 4.3 while.25
  158.9 19.7 %custom-call.20 = f32[2,128,128]{1,2,0:T(8,128)S(1)} custom-call(f32[2,128,128]{2,1,0:T(8,128)S(1)} %get-tuple-element.28), custom_call_target="InvertDiagBlocksLowerTriangular" | custom-call | tf_op jit(solution)/shard_map/jit(_solve_triangular)/triangular_solve | solution.py:23
  190.9 4.5 fusion.3
  195.7 124.0 %all-gather.5.cloned.1.call-done = f32[4096,512]{1,0:T(8,128)} async-done(((f32[512,512]{1,0:T(8,128)}), f32[4096,512]{1,0:T(8,128)}) %all-gather.5.cloned.1.call-update) | async-done | bytes 8388624 | tf_op jit(solution)/shard_map/all_gather | solution.py:56
  319.6 5.5 reduce_sum.401
  333.9 11.7 cholesky.248
  345.7 10.4 custom-call.35
  358.3 12.1 cholesky.265
  374.2 5.5 while.26
  380.3 20.5 %custom-call.36 = f32[2,128,128]{1,2,0:T(8,128)S(1)} custom-call(f32[2,128,128]{2,1,0:T(8,128)} %copy-done.15), custom_call_target="InvertDiagBlocksLowerTriangular" | custom-call | tf_op jit(solution)/shard_map/jit(_solve_triangular)/triangular_solve | solution.py:23
  402.2 4.1 fusion.2
  407.8 23.0 %collective-permute-done.1 = f32[256,1024]{1,0:T(8,128)} collective-permute-done((f32[256,1024]{1,0:T(8,128)}, f32[256,1024]{1,0:T(8,128)}, u32[]{:S(2)}, u32[]{:S(2)}) %collective-permute-start.1) | collective-permute-done | bytes 1048608 | tf_op jit(solution)/shard_map/ppermute | solution.py:15
  433.9 4.5 fusion.1
  438.9 5.8 psum.442
  444.7 117.3 %all-gather.7.cloned.1.call-done = f32[4096,512]{1,0:T(8,128)} async-done(((f32[512,512]{1,0:T(8,128)}), f32[4096,512]{1,0:T(8,128)}) %all-gather.7.cloned.1.call-update) | async-done | bytes 8388624 | tf_op jit(solution)/shard_map/all_gather | solution.py:56
  561.9 5.5 reduce_sum.403
  576.2 11.7 cholesky.282
  588.0 10.4 custom-call.37
  600.6 11.9 cholesky.299
  616.3 5.5 while.27
  622.4 20.5 %custom-call.38 = f32[2,128,128]{1,2,0:T(8,128)S(1)} custom-call(f32[2,128,128]{2,1,0:T(8,128)} %copy-done.16), custom_call_target="InvertDiagBlocksLowerTriangular" | custom-call | tf_op jit(solution)/shard_map/jit(_solve_triangular)/triangular_solve | solution.py:23
  653.0 18.9 %psum.445 = f32[256]{0:T(256)S(1)} all-reduce(f32[256]{0:T(256)S(1)} %bitcast.785), channel_id=1, replica_groups=mesh['rows'=4,'cols'=8] {'cols'}, use_global_device_ids=true, to_apply=%region_13.16 | all-reduce | flops 256 | bytes 2048 | tf_op jit(solution)/shard_map/psum | solution.py:67
  672.0 47.7 %all-reduce.34.cloned.1.call-done = f32[256,256]{0,1:T(8,128)} async-done(((f32[256,256]{0,1:T(8,128)}), f32[256,256]{0,1:T(8,128)}) %all-reduce.34.cloned.1.call-update) | async-done | bytes 262160 | tf_op jit(solution)/shard_map/psum | solution.py:60
  721.8 11.7 cholesky.316
  733.5 9.8 custom-call.39
  743.8 11.7 cholesky.333
  758.2 5.4 while.28
  763.7 19.8 %custom-call.40 = f32[2,128,128]{1,2,0:T(8,128)S(1)} custom-call(f32[2,128,128]{2,1,0:T(8,128)S(1)} %get-tuple-element.91), custom_call_target="InvertDiagBlocksLowerTriangular" | custom-call | tf_op jit(solution)/shard_map/jit(_cho_solve)/triangular_solve | solution.py:70
  787.8 20.6 %all-reduce.19 = (f32[1024]{0:T(1024)S(1)}, f32[]{:T(128)}, f32[]{:T(128)}) all-reduce(f32[1024]{0:T(1024)S(1)} %bitcast.764, f32[]{:T(128)} %get-tuple-element.250, f32[]{:T(128)} %get-tuple-element.248), channel_id=1, replica_groups=mesh['rows'=4,'cols'=8] {'cols'}, use_global_device_ids=true, to_apply=%region_17.21 | all-reduce | flops 1026 | bytes 8208 | tf_op jit(solution)/shard_map/psum | solution.py:77
  810.0 6.4 all-reduce.28
  821.9 17.8 %all-reduce.18 = (f32[256]{0:T(256)S(1)}, f32[]{:T(128)}) all-reduce(f32[256]{0:T(256)S(1)} %bitcast.796, f32[]{:T(128)} %get-tuple-element.244), channel_id=1, replica_groups=mesh['rows'=4,'cols'=8] {'cols'}, use_global_device_ids=true, to_apply=%region_25.29 | all-reduce | flops 257 | bytes 2056 | tf_op jit(solution)/shard_map/psum | solution.py:67
  845.9 20.0 %all-reduce.17 = (f32[1024]{0:T(1024)S(1)}, f32[]{:T(128)}) all-reduce(f32[1024]{0:T(1024)S(1)} %bitcast.766, f32[]{:T(128)} %get-tuple-element.242), channel_id=1, replica_groups=mesh['rows'=4,'cols'=8] {'cols'}, use_global_device_ids=true, to_apply=%region_27.31 | all-reduce | flops 1025 | bytes 8200 | tf_op jit(solution)/shard_map/psum | solution.py:77
  867.0 6.4 all-reduce.27
  877.4 17.8 %all-reduce.16 = (f32[256]{0:T(256)S(1)}, f32[]{:T(128)}) all-reduce(f32[256]{0:T(256)S(1)} %bitcast.797, f32[]{:T(128)} %get-tuple-element.238), channel_id=1, replica_groups=mesh['rows'=4,'cols'=8] {'cols'}, use_global_device_ids=true, to_apply=%region_35.39 | all-reduce | flops 257 | bytes 2056 | tf_op jit(solution)/shard_map/psum | solution.py:67
  901.5 20.0 %all-reduce.15 = (f32[1024]{0:T(1024)S(1)}, f32[]{:T(128)}) all-reduce(f32[1024]{0:T(1024)S(1)} %bitcast.768, f32[]{:T(128)} %get-tuple-element.236), channel_id=1, replica_groups=mesh['rows'=4,'cols'=8] {'cols'}, use_global_device_ids=true, to_apply=%region_37.41 | all-reduce | flops 1025 | bytes 8200 | tf_op jit(solution)/shard_map/psum | solution.py:77
  922.6 6.4 all-reduce.26
  933.0 18.0 %all-reduce.14 = (f32[256]{0:T(256)S(1)}, f32[]{:T(128)}) all-reduce(f32[256]{0:T(256)S(1)} %bitcast.798, f32[]{:T(128)} %get-tuple-element.232), channel_id=1, replica_groups=mesh['rows'=4,'cols'=8] {'cols'}, use_global_device_ids=true, to_apply=%region_45.49 | all-reduce | flops 257 | bytes 2056 | tf_op jit(solution)/shard_map/psum | solution.py:67
  959.0 20.0 %all-reduce.13 = (f32[1024]{0:T(1024)S(1)}, f32[]{:T(128)}) all-reduce(f32[1024]{0:T(1024)S(1)} %bitcast.770, f32[]{:T(128)} %get-tuple-element.230), channel_id=1, replica_groups=mesh['rows'=4,'cols'=8] {'cols'}, use_global_device_ids=true, to_apply=%region_47.51 | all-reduce | flops 1025 | bytes 8200 | tf_op jit(solution)/shard_map/psum | solution.py:77
  980.0 6.4 all-reduce.25
  990.5 17.8 %all-reduce.12 = (f32[256]{0:T(256)S(1)}, f32[]{:T(128)}) all-reduce(f32[256]{0:T(256)S(1)} %bitcast.799, f32[]{:T(128)} %get-tuple-element.226), channel_id=1, replica_groups=mesh['rows'=4,'cols'=8] {'cols'}, use_global_device_ids=true, to_apply=%region_55.59 | all-reduce | flops 257 | bytes 2056 | tf_op jit(solution)/shard_map/psum | solution.py:67
  1016.2 20.0 %all-reduce.11 = (f32[1024]{0:T(1024)S(1)}, f32[]{:T(128)}) all-reduce(f32[1024]{0:T(1024)S(1)} %bitcast.772, f32[]{:T(128)} %get-tuple-element.224), channel_id=1, replica_groups=mesh['rows'=4,'cols'=8] {'cols'}, use_global_device_ids=true, to_apply=%region_57.61 | all-reduce | flops 1025 | bytes 8200 | tf_op jit(solution)/shard_map/psum | solution.py:77
  1037.3 6.4 all-reduce.24
  1047.7 17.8 %all-reduce.10 = (f32[256]{0:T(256)S(1)}, f32[]{:T(128)}) all-reduce(f32[256]{0:T(256)S(1)} %bitcast.800, f32[]{:T(128)} %get-tuple-element.220), channel_id=1, replica_groups=mesh['rows'=4,'cols'=8] {'cols'}, use_global_device_ids=true, to_apply=%region_65.69 | all-reduce | flops 257 | bytes 2056 | tf_op jit(solution)/shard_map/psum | solution.py:67
  1073.4 20.0 %all-reduce.9 = (f32[1024]{0:T(1024)S(1)}, f32[]{:T(128)}) all-reduce(f32[1024]{0:T(1024)S(1)} %bitcast.774, f32[]{:T(128)} %get-tuple-element.218), channel_id=1, replica_groups=mesh['rows'=4,'cols'=8] {'cols'}, use_global_device_ids=true, to_apply=%region_67.71 | all-reduce | flops 1025 | bytes 8200 | tf_op jit(solution)/shard_map/psum | solution.py:77
  1094.5 6.4 all-reduce.23
  1105.0 17.8 %all-reduce.8 = (f32[256]{0:T(256)S(1)}, f32[]{:T(128)}) all-reduce(f32[256]{0:T(256)S(1)} %bitcast.801, f32[]{:T(128)} %get-tuple-element.214), channel_id=1, replica_groups=mesh['rows'=4,'cols'=8] {'cols'}, use_global_device_ids=true, to_apply=%region_75.79 | all-reduce | flops 257 | bytes 2056 | tf_op jit(solution)/shard_map/psum | solution.py:67
  1130.7 20.0 %all-reduce.7 = (f32[1024]{0:T(1024)S(1)}, f32[]{:T(128)}) all-reduce(f32[1024]{0:T(1024)S(1)} %bitcast.776, f32[]{:T(128)} %get-tuple-element.212), channel_id=1, replica_groups=mesh['rows'=4,'cols'=8] {'cols'}, use_global_device_ids=true, to_apply=%region_77.81 | all-reduce | flops 1025 | bytes 8200 | tf_op jit(solution)/shard_map/psum | solution.py:77
  1151.8 6.5 all-reduce.22
  1162.4 18.0 %all-reduce.6 = (f32[256]{0:T(256)S(1)}, f32[]{:T(128)}) all-reduce(f32[256]{0:T(256)S(1)} %bitcast.802, f32[]{:T(128)} %get-tuple-element.208), channel_id=1, replica_groups=mesh['rows'=4,'cols'=8] {'cols'}, use_global_device_ids=true, to_apply=%region_85.89 | all-reduce | flops 257 | bytes 2056 | tf_op jit(solution)/shard_map/psum | solution.py:67
  1188.3 20.0 %all-reduce.5 = (f32[1024]{0:T(1024)S(1)}, f32[]{:T(128)}) all-reduce(f32[1024]{0:T(1024)S(1)} %bitcast.778, f32[]{:T(128)} %get-tuple-element.206), channel_id=1, replica_groups=mesh['rows'=4,'cols'=8] {'cols'}, use_global_device_ids=true, to_apply=%region_87.91 | all-reduce | flops 1025 | bytes 8200 | tf_op jit(solution)/shard_map/psum | solution.py:77
  1209.4 6.5 all-reduce.21
  1220.0 17.8 %all-reduce.4 = (f32[256]{0:T(256)S(1)}, f32[]{:T(128)}) all-reduce(f32[256]{0:T(256)S(1)} %bitcast.803, f32[]{:T(128)} %get-tuple-element.202), channel_id=1, replica_groups=mesh['rows'=4,'cols'=8] {'cols'}, use_global_device_ids=true, to_apply=%region_95.99 | all-reduce | flops 257 | bytes 2056 | tf_op jit(solution)/shard_map/psum | solution.py:67
  1245.7 20.0 %all-reduce.3 = (f32[1024]{0:T(1024)S(1)}, f32[]{:T(128)}) all-reduce(f32[1024]{0:T(1024)S(1)} %bitcast.780, f32[]{:T(128)} %get-tuple-element.200), channel_id=1, replica_groups=mesh['rows'=4,'cols'=8] {'cols'}, use_global_device_ids=true, to_apply=%region_97.101 | all-reduce | flops 1025 | bytes 8200 | tf_op jit(solution)/shard_map/psum | solution.py:77
  1266.7 6.5 all-reduce.20
  1277.3 17.8 %all-reduce.2 = (f32[256]{0:T(256)S(1)}, f32[]{:T(128)}) all-reduce(f32[256]{0:T(256)S(1)} %bitcast.804, f32[]{:T(128)} %get-tuple-element.196), channel_id=1, replica_groups=mesh['rows'=4,'cols'=8] {'cols'}, use_global_device_ids=true, to_apply=%region_105.109 | all-reduce | flops 257 | bytes 2056 | tf_op jit(solution)/shard_map/psum | solution.py:67
  1303.1 20.0 %all-reduce.1 = (f32[1024]{0:T(1024)S(1)}, f32[]{:T(128)}) all-reduce(f32[1024]{0:T(1024)S(1)} %bitcast.782, f32[]{:T(128)} %get-tuple-element.194), channel_id=1, replica_groups=mesh['rows'=4,'cols'=8] {'cols'}, use_global_device_ids=true, to_apply=%region_107.111 | all-reduce | flops 1025 | bytes 8200 | tf_op jit(solution)/shard_map/psum | solution.py:77
  1323.8 6.5 psum.502
  (340 shorter events, 184.0 us)
Async XLA Ops:
  7.2 26.4 %copy-start = (bf16[1024,256]{1,0:T(8,128)(2,1)S(1)}, bf16[1024,256]{1,0:T(8,128)(2,1)}, u32[]{:S(2)}) copy-start(bf16[1024,256]{1,0:T(8,128)(2,1)} %param.15) | copy-start | bytes 1572868
  7.2 26.4 %copy-start.10 = (f32[1024]{0:T(1024)S(1)}, f32[1024]{0:T(1024)}, u32[]{:S(2)}) copy-start(f32[1024]{0:T(1024)} %param.13) | copy-start | bytes 12292
  7.2 26.4 %copy-start.1 = (bf16[1024,1024]{1,0:T(8,128)(2,1)S(1)}, bf16[1024,1024]{1,0:T(8,128)(2,1)}, u32[]{:S(2)}) copy-start(bf16[1024,1024]{1,0:T(8,128)(2,1)} %param.11) | copy-start | bytes 6291460
  7.2 26.3 %copy-start.18 = (s32[1024]{0:T(1024)S(1)}, s32[1024]{0:T(1024)}, u32[]{:S(2)}) copy-start(s32[1024]{0:T(1024)} %param.14) | copy-start | bytes 12292
  7.2 105.5 %all-reduce.32.cloned.1.call-start = ((), (), s32[]{:S(2)}) async-start(), calls=%async_computation | async-start | bytes 2097152 | tf_op jit(solution)/shard_map/psum | solution.py:43
  36.9 282.7 %all-gather.5.cloned.1.call-start = ((), (), s32[]{:S(2)}) async-start(), calls=%async_computation.2 | async-start | bytes 9437184 | tf_op jit(solution)/shard_map/all_gather | solution.py:56
  158.9 19.7 %copy-start.19 = (s32[2,2]{1,0:T(2,128)}, s32[2,2]{1,0:T(2,128)S(1)}, u32[]{:S(2)}) copy-start(s32[2,2]{1,0:T(2,128)S(1)} %get-tuple-element.492) | copy-start | bytes 52
  184.8 3.0 collective-permute-start
  189.5 1.1 copy-start.7
  189.5 1.3 copy-start.9
  195.4 366.5 %all-gather.7.cloned.1.call-start = ((), (), s32[]{:S(2)}) async-start(), calls=%async_computation.3 | async-start | bytes 9437184 | tf_op jit(solution)/shard_map/all_gather | solution.py:56
  333.2 0.7 copy-start.13
  370.4 2.7 copy-start.11
  379.6 0.6 copy-start.15
  400.8 1.5 copy-start.8
  406.3 24.5 %collective-permute-start.1 = (f32[256,1024]{1,0:T(8,128)}, f32[256,1024]{1,0:T(8,128)}, u32[]{:S(2)}, u32[]{:S(2)}) collective-permute-start(f32[256,1024]{1,0:T(8,128)} %fusion.2), channel_id=1, source_target_pairs={{0,16},{8,24},{16,0},{24,8},{1,17},{9,25},{17,1},{25,9},{2,18},{10... | collective-permute-start | bytes 3145736 | tf_op jit(solution)/shard_map/ppermute | solution.py:15
  432.6 1.1 copy-start.4
  432.6 1.3 copy-start.6
  438.4 281.2 %all-reduce.34.cloned.1.call-start = ((), (), s32[]{:S(2)}) async-start(), calls=%async_computation.1 | async-start | bytes 524288 | tf_op jit(solution)/shard_map/psum | solution.py:60
  575.5 0.7 copy-start.14
  612.5 2.7 copy-start.12
  621.7 0.6 copy-start.16
  642.9 1.5 copy-start.5
  647.5 1.0 copy-start.2
  648.4 1.8 copy-start.17
  763.7 132.3 %copy-start.3 = (f32[256,256]{1,0:T(8,128)}, f32[256,256]{1,0:T(8,128)S(1)}, u32[]{:S(2)}) copy-start(f32[256,256]{1,0:T(8,128)S(1)} %get-tuple-element.476) | copy-start | bytes 786436
Sparse Core Ops, SparseCore 0:
  37.0 75.6 all-reduce.31
  195.5 124.0 all-gather.4
  438.5 123.3 all-gather.6
  650.3 69.2 all-reduce.33
